TPU v7x, 256 devices: a 2x2x32 block of a 4x8x32 slice. The times are simulated.
256 devices in a mesh: grp: 4 (over x, y), tp: 32 (over z), tower: 2 (over core).
Axes of the slice: x: 2, y: 2, z: 32, core: 2. Of those that a mesh axis runs over, the one named last changes fastest.
The devices are a block of a 4x8x32 slice.
Arguments:
- hidden: bfloat16 [2, 4096, 3072], P('tower', ('grp', 'tp')), parts along dimension 1, may hold values from -6 to 6
- modulation: float32 [2, 3, 3072], P('tower'), may hold values from -3 to 7, as said below
- qk_gains: float32 [2, 3, 4096], P('tower', None, 'tp'), may hold values from 0.75 to 13
- counts: int32 [2, 4], P(None, 'grp'), parts along dimension 1, may hold values from 256 to 1024
- offsets: int32 [2, 4], P(None, 'grp'), parts along dimension 1, may hold values from 0 to 8191
- in_weights: bfloat16 [2, 3072, 4, 4096], P('tower', None, None, 'tp'), may hold values from -0.109375 to 0.109375
- out_weights: bfloat16 [2, 2, 4096, 3072], P('tower', None, 'tp'), may hold values from -0.5 to 0.5
Outputs:
- updated: bfloat16 [2, 4096, 3072], P('tower', ('grp', 'tp')), parts along dimension 1
There are 4 independent parts, one for each index of `grp`. A program takes and returns all parts, laid end to end along the dimension named above; an argument that names none is the same for every part. Nothing has to cross between parts.
Inputs may be any that keep to these rules, and one draw needn't show every extreme that they name: `modulation`: rows are shift, scale and gate.
All inputs are finite; a program needn't handle non-finite values.
Results may differ from a plain program's by a relative error of at most 0.025.
The roundings to bfloat16 on the way count: a program that leaves them out, or rounds other values in their place, can miss the bound.
Values may be sent and summed in bfloat16 or wider, within the bound.
No kernel may reach another device: no remote copies, remote signals or barrier semaphores. Data moves between devices by JAX's collectives and lax.ppermute only.
A program may use at most 64 MiB of HBM per device.

v0:
```python
import math
import jax
import jax.numpy as jnp
from jax import lax
from jax.sharding import PartitionSpec as P

epsilon = 1e-06
rope_base = 10000.0
masked_score = -1e30


def partner(value, axis, distance):
    mask = 2**distance
    pairs = [(source, source ^ mask) for source in range(lax.axis_size(axis))]
    return lax.ppermute(value, axis, pairs)


def layer_norm(states):
    centre = states - jnp.mean(states, -1, keepdims=True)
    spread = jnp.mean(centre * centre, -1, keepdims=True)
    return centre * lax.rsqrt(spread + epsilon)


def rotate(columns, positions):
    head_width = columns.shape[-1]
    pair_index = jnp.arange(head_width // 2, dtype=jnp.int32)
    frequency = jnp.exp(pair_index.astype(jnp.float32) * (-2.0 * math.log(rope_base) / head_width))
    angles = positions.reshape((positions.shape[0],) + (1,) * (columns.ndim - 1)) * frequency
    cosine = jnp.cos(angles)
    sine_table = jnp.sin(angles)
    even_part = columns[..., 0::2]
    odd_part = columns[..., 1::2]
    turned = jnp.stack(
        [even_part * cosine - odd_part * sine_table, even_part * sine_table + odd_part * cosine], -1
    )
    return turned.reshape(columns.shape)


def finish(projected, head_gains, positions):
    query_like = jnp.stack([projected[:, 0], projected[:, 1], projected[:, 3]], 1)
    squares = jnp.mean(query_like * query_like, -1, keepdims=True)
    query_like = query_like * lax.rsqrt(squares + epsilon) * head_gains[None]
    turned = rotate(query_like, positions)
    return jnp.stack([turned[:, 0], turned[:, 1], projected[:, 2], turned[:, 2]], 1)


def attend(queries, key_rows, value_rows, key_count):
    scores = jnp.einsum("qd,kd->qk", queries, key_rows, preferred_element_type=jnp.float32) * (
        1.0 / math.sqrt(queries.shape[-1])
    )
    usable = jnp.arange(key_rows.shape[0], dtype=jnp.int32) < key_count
    scores = jnp.where(usable[None, :], scores, masked_score)
    row_max = jnp.max(scores, -1, keepdims=True)
    raised = jnp.exp(scores - row_max)
    attention = (raised / jnp.sum(raised, -1, keepdims=True)).astype(jnp.bfloat16)
    return jnp.dot(attention, value_rows, preferred_element_type=jnp.float32).astype(jnp.bfloat16)


def attend_blocks(queries, key_rows, value_rows, key_count):
    row_count = queries.shape[0]
    block_rows = min(512, row_count)
    grouped = queries.reshape(row_count // block_rows, block_rows, queries.shape[-1])
    result = lax.map(
        lambda query_block: attend(query_block, key_rows, value_rows, key_count), grouped
    )
    return result.reshape(row_count, queries.shape[-1])


def local(hidden, modulation, qk_gains, counts, offsets, in_weights, out_weights):
    states = hidden[0].astype(jnp.float32)
    modulate = modulation[0]
    normed = (layer_norm(states) * (1.0 + modulate[1]) + modulate[0]).astype(jnp.bfloat16)
    local_rows = states.shape[0]
    model_width = normed.shape[1]
    all_rows = local_rows * lax.axis_size("tp")
    tower_index = lax.axis_index("tower")
    own_count = lax.dynamic_index_in_dim(counts[:, 0], tower_index, 0, False)
    own_offset = lax.dynamic_index_in_dim(offsets[:, 0], tower_index, 0, False)
    head_width = in_weights.shape[-1]
    flat_weights = in_weights[0].reshape(model_width, 4 * head_width)
    head_gains = qk_gains[0].reshape(3, 1, head_width)
    row_piece = lax.all_gather(normed, "tp", axis=0, tiled=True)
    row_count = row_piece.shape[0]
    projected = jnp.dot(row_piece, flat_weights, preferred_element_type=jnp.float32).reshape(
        row_count, 4, 1, head_width
    )
    positions = (own_offset + jnp.arange(row_count, dtype=jnp.int32)).astype(jnp.float32)
    finished = finish(projected, head_gains, positions)
    projected = (
        finished.astype(jnp.bfloat16)
        .reshape(row_count, 4 * head_width)
        .reshape(all_rows, 4, head_width)
    )
    queries = projected[:, 0]
    key_rows = projected[:, 1]
    value_rows = projected[:, 2]
    cross_queries = projected[:, 3]
    self_out = attend_blocks(queries, key_rows, value_rows, own_count)
    foreign = partner(cross_queries, "tower", 0)
    answered = attend_blocks(foreign, key_rows, value_rows, own_count)
    cross_out = partner(answered, "tower", 0)
    both_out = jnp.concatenate([self_out, cross_out], 1)
    flat_out = out_weights[0].reshape(2 * head_width, model_width)
    branch = lax.psum_scatter(
        jnp.dot(both_out, flat_out, preferred_element_type=jnp.float32).astype(jnp.bfloat16),
        "tp",
        scatter_dimension=0,
        tiled=True,
    ).astype(jnp.float32)
    return (states + modulate[2] * branch).astype(jnp.bfloat16)[None]


def solution(mesh):
    return jax.shard_map(
        local,
        mesh=mesh,
        in_specs=(
            P("tower", ("grp", "tp"), None),
            P("tower", None, None),
            P("tower", None, "tp"),
            P(None, "grp"),
            P(None, "grp"),
            P("tower", None, None, "tp"),
            P("tower", None, "tp", None),
        ),
        out_specs=P("tower", ("grp", "tp"), None),
        check_vma=False,
    )
```

profile of v0, /device:TPU:38, one launch (start us, length us, event | category | flops | bytes accessed | tf_op | source)
XLA Modules:
  0.0 345.4 jit_solution(10798262315295197064)
XLA Ops:
  6.6 0.9 fusion.41
  7.4 1.1 convert_reduce_fusion
  8.5 1.2 fusion.32
  9.7 1.8 fusion.35
  11.6 4.1 %copy.25 = bf16[384,8,4,128]{3,1,2,0:T(8,128)(2,1)} copy(bf16[384,8,4,128]{3,2,1,0:T(4,128)(2,1)} %bitcast.111) | data formatting | bytes 6291456
  15.6 4.8 %copy.11 = bf16[512,3072]{1,0:T(8,128)(2,1)} copy(bf16[512,3072]{0,1:T(8,128)(2,1)} %bitcast.108) | data formatting | bytes 6291456 | tf_op jit(solution)/shard_map/dot_general | solution.py:84
  22.3 1.8 multiply_cosine_fusion
  24.1 142.7 %all-gather.2.cloned.1.call-done = bf16[1024,3072]{1,0:T(8,128)(2,1)} async-done(((bf16[32,3072]{1,0:T(8,128)(2,1)}), bf16[1024,3072]{1,0:T(8,128)(2,1)}) %all-gather.2.cloned.1.call-update) | async-done | bytes 6291472 | tf_op jit(solution)/shard_map/all_gather | solution.py:82
  166.8 6.5 %fusion.22 = f32[1024,4,1,128]{0,3,1,2:T(8,128)S(1)} fusion(bf16[4,128,3072]{2,1,0:T(8,128)(2,1)} %bitcast.112, bf16[1024,3072]{1,0:T(8,128)(2,1)} %all-gather.2.cloned.1.call-done), kind=kOutput, calls=%fused_computation.34 | convolution fusion | flops 3221225472 | bytes 11534336 | tf_op jit(solution)/shard_map/dot_general | solution.py:84
  173.6 1.1 copy-done.2
  174.9 2.2 slice.56
  177.1 2.1 slice.55
  179.2 1.7 subtract_bitcast_fusion
  181.0 0.8 copy.12
  182.6 1.1 fusion.37
  184.2 5.1 %while.21 = (s32[]{:T(128)}, bf16[2,512,128]{2,1,0:T(8,128)(2,1)S(1)}, s32[]{:T(128)}, bf16[2,512,128]{2,1,0:T(8,128)(2,1)S(1)}, bf16[1024,128]{1,0:T(8,128)(2,1)S(1)}, /*index=5*/bf16[1024,128]{1,0:T(8,128)(2,1)S(1)}, s32[]{:T(128)}) while((s32[]{:T(128)}, bf16[2,512,128]{2,1,0:T(8,128)(2,1)S(1)}, s32[]{:T(128)}, ...), condition=%wide.region_10.11_spmd, body=%wide.region_7.10_spmd.sunk | while | flops 274792448 | bytes 7092321 | solution.py:63
  186.1 0.7 fusion.67
  188.6 0.7 fusion.67
  189.3 0.8 collective-permute-start.1
  190.2 5.1 %while.20 = (s32[]{:T(128)}, bf16[2,512,128]{2,1,0:T(8,128)(2,1)S(1)}, s32[]{:T(128)}, bf16[2,512,128]{2,1,0:T(8,128)(2,1)S(1)}, bf16[1024,128]{1,0:T(8,128)(2,1)S(1)}, /*index=5*/bf16[1024,128]{1,0:T(8,128)(2,1)S(1)}, s32[]{:T(128)}) while((s32[]{:T(128)}, bf16[2,512,128]{2,1,0:T(8,128)(2,1)S(1)}, s32[]{:T(128)}, ...), condition=%wide.region_6.7_spmd, body=%wide.region_3.6_spmd.sunk | while | flops 274792448 | bytes 7092321 | solution.py:63
  194.5 0.7 fusion.62
  195.3 4.5 %convolution_convert_fusion.2 = bf16[1024,3072]{1,0:T(8,128)(2,1)} fusion(bf16[256,3072]{1,0:T(8,128)(2,1)S(1)} %bitcast.107, bf16[1024,128]{1,0:T(8,128)(2,1)S(1)} %collective-permute-done.1, bf16[1024,128]{1,0:T(8,128)(2,1)S(1)} %bitcast.113), kind=kOutput, calls=%fused_computation.32 | convolution fusion | flops 1614807040 | bytes 8388608 | tf_op jit(solution)/shard_map/dot_general | solution.py:105
  199.8 137.0 %reduce-scatter.2.cloned.1.call-done = bf16[32,3072]{1,0:T(8,128)(2,1)} async-done(((bf16[1024,3072]{1,0:T(8,128)(2,1)}), bf16[32,3072]{1,0:T(8,128)(2,1)}) %reduce-scatter.2.cloned.1.call-update) | async-done | bytes 196624 | tf_op jit(solution)/shard_map/reduce_scatter | solution.py:104
  336.9 1.7 fusion.38
  (54 shorter events, 12.0 us)
Async XLA Ops:
  6.5 188.7 %copy-start = (bf16[1,2,128,3072]{3,2,1,0:T(8,128)(2,1)S(1)}, bf16[1,2,128,3072]{3,2,1,0:T(8,128)(2,1)}, u32[]{:S(2)}) copy-start(bf16[1,2,128,3072]{3,2,1,0:T(8,128)(2,1)} %param.17) | copy-start | bytes 4718596
  6.6 160.3 %all-gather.2.cloned.1.call-start = ((), (), s32[]{:S(2)}) async-start(), calls=%async_computation.1 | async-start | bytes 6488064 | tf_op jit(solution)/shard_map/all_gather | solution.py:82
  11.5 325.4 %reduce-scatter.2.cloned.1.call-start = ((), (), s32[]{:S(2)}) async-start(), calls=%async_computation.2 | async-start | bytes 6488064 | tf_op jit(solution)/shard_map/reduce_scatter | solution.py:104
  15.6 4.8 %copy-start.3 = (f32[1,3,128]{2,0,1:T(1,128)S(1)}, f32[1,3,128]{2,0,1:T(1,128)}, u32[]{:S(2)}) copy-start(f32[1,3,128]{2,0,1:T(1,128)} %param.13) | copy-start | bytes 4612
  15.6 4.8 %copy-start.4 = (s32[2,1]{0,1:T(1,128)S(1)}, s32[2,1]{0,1:T(1,128)}, u32[]{:S(2)}) copy-start(s32[2,1]{0,1:T(1,128)} %param.14) | copy-start | bytes 28
  15.6 5.5 %copy-start.5 = (s32[2,1]{0,1:T(1,128)S(1)}, s32[2,1]{0,1:T(1,128)}, u32[]{:S(2)}) copy-start(s32[2,1]{0,1:T(1,128)} %param.15) | copy-start | bytes 28
  173.4 1.4 copy-start.2
  182.2 1.8 collective-permute-start
  189.3 5.9 %collective-permute-start.1 = (bf16[1024,128]{1,0:T(8,128)(2,1)S(1)}, bf16[1024,128]{1,0:T(8,128)(2,1)S(1)}, u32[]{:S(2)}, u32[]{:S(2)}) collective-permute-start(bf16[1024,128]{1,0:T(8,128)(2,1)S(1)} %bitcast.114), channel_id=1, source_target_pairs={{0,1},{1,0},{2,3},{3,2},{4,5},{5,4},{6,7},{7,6},{8,9},{9,8},{10,11... | collective-permute-start | bytes 786440 | tf_op jit(solution)/shard_map/ppermute | solution.py:15
  199.7 137.1 %copy-start.1 = (bf16[1,32,3072]{2,1,0:T(8,128)(2,1)S(1)}, bf16[1,32,3072]{2,1,0:T(8,128)(2,1)}, u32[]{:S(2)}) copy-start(bf16[1,32,3072]{2,1,0:T(8,128)(2,1)} %param.11) | copy-start | bytes 589828
Sparse Core Ops, SparseCore 0:
  11.6 155.1 all-gather.1
  199.9 136.8 reduce-scatter.1
where the time goes:
time: 346 us; the launch traced here: 345 us
  waiting for transfers between devices  280 us (81%)
  local copies, waits for them, and re-layouts  18.6 us (5%)
  other arithmetic  16.2 us (5%)
  matrix products  16 us (5%)
  between operations  13.6 us (4%)
    all_gather x1, waiting for transfers between devices, local(): row_piece = lax.all_gather(normed, 'tp', axis=0, tiled=True)  143 us
    reduce_scatter x1, waiting for transfers between devices, local(): lax.psum_scatter(jnp.dot(both_out, flat_out, preferred_element_type=jnp.f...  137 us
  transfers between devices with their start and end apart: 4, of which 2 were waited for; matrix products, arithmetic and copies ran while one was open for 6% of the time, Pallas kernels for 0%

commit v1 on v0

--- a/solution.py
+++ b/solution.py
@@ -7,6 +7,12 @@
 epsilon = 1e-06
 rope_base = 10000.0
 masked_score = -1e30
+
+
+def tiled_gather(x, axis, dim):
+    length = lax.axis_size(axis)
+    repeats = [length if d == dim else 1 for d in range(x.ndim)]
+    return lax.all_to_all(jnp.tile(x, repeats), axis, split_axis=dim, concat_axis=dim, tiled=True)
 
 
 def partner(value, axis, distance):
@@ -79,7 +85,7 @@
     head_width = in_weights.shape[-1]
     flat_weights = in_weights[0].reshape(model_width, 4 * head_width)
     head_gains = qk_gains[0].reshape(3, 1, head_width)
-    row_piece = lax.all_gather(normed, "tp", axis=0, tiled=True)
+    row_piece = tiled_gather(normed, "tp", 0)
     row_count = row_piece.shape[0]
     projected = jnp.dot(row_piece, flat_weights, preferred_element_type=jnp.float32).reshape(
         row_count, 4, 1, head_width

time: 346 us -> 776 us (2.24)
  waiting for transfers between devices: 280 us -> 674 us
  starting transfers between devices: 0.99 us -> 33.7 us
    all_to_all x0 -> x1, waiting for transfers between devices: none -> 532 us  [tiled_gather(): lax.all_to_all(jnp.tile(x, repeats), axis, split_axis=dim, concat_axis=di...]
    all_gather x1 -> x0, waiting for transfers between devices: 143 us -> none  [local(): row_piece = lax.all_gather(normed, 'tp', axis=0, tiled=True)]
    all_to_all x0 -> x1, starting transfers between devices: none -> 32.7 us  [tiled_gather(): lax.all_to_all(jnp.tile(x, repeats), axis, split_axis=dim, concat_axis=di...]
  transfers between devices with their start and end apart: 4 -> 4, of which waited for: 2 -> 2; matrix products, arithmetic and copies ran while one was open for 6% -> 2% of each run, Pallas kernels for 0% -> 0%
where the time goes in v1:
time: 776 us; the launch traced here: 775 us
  waiting for transfers between devices  674 us (87%)
  starting transfers between devices  33.7 us (4%)
  local copies, waits for them, and re-layouts  22 us (3%)
  matrix products  16 us (2%)
  other arithmetic  15.2 us (2%)
  between operations  13.7 us (2%)
    all_to_all x1, waiting for transfers between devices, tiled_gather(): lax.all_to_all(jnp.tile(x, repeats), axis, split_axis=dim, concat_axis=di...  532 us
    reduce_scatter x1, waiting for transfers between devices, local(): lax.psum_scatter(jnp.dot(both_out, flat_out, preferred_element_type=jnp.f...  142 us
    all_to_all x1, starting transfers between devices, tiled_gather(): lax.all_to_all(jnp.tile(x, repeats), axis, split_axis=dim, concat_axis=di...  32.7 us
  transfers between devices with their start and end apart: 4, of which 2 were waited for; matrix products, arithmetic and copies ran while one was open for 2% of the time, Pallas kernels for 0%

profile of v1, /device:TPU:38, one launch (start us, length us, event | category | flops | bytes accessed | tf_op | source)
XLA Modules:
  0.0 774.9 jit_solution(1505417734129079386)
XLA Ops:
  6.6 0.9 fusion.36
  7.4 1.1 convert_reduce_fusion
  8.5 1.2 fusion.27
  9.7 1.1 fusion.30
  10.7 3.4 tile.2
  14.2 32.7 %all-to-all-start = ((bf16[32,32,3072]{2,1,0:T(8,128)(2,1)}), bf16[32,32,3072]{2,1,0:T(8,128)(2,1)}, u32[]{:S(2)}, u32[]{:S(2)}) async-start(bf16[32,32,3072]{2,1,0:T(8,128)(2,1)} %tile.2), calls=%async_computation | async-start | bytes 12582912 | tf_op jit(solution)/shard_map/all_to_all | solution.py:15
  46.9 4.1 copy.25
  51.0 4.7 copy.11
  57.7 1.8 multiply_cosine_fusion
  59.4 532.4 %all-to-all-done = bf16[32,32,3072]{2,1,0:T(8,128)(2,1)} async-done(((bf16[32,32,3072]{2,1,0:T(8,128)(2,1)}), bf16[32,32,3072]{2,1,0:T(8,128)(2,1)}, u32[]{:S(2)}, u32[]{:S(2)}) %all-to-all-start) | async-done | bytes 6291488 | tf_op jit(solution)/shard_map/all_to_all | solution.py:15
  591.8 6.5 convolution_bitcast_fusion
  598.6 1.1 copy-done.2
  599.9 2.1 slice.55
  602.0 2.2 slice.56
  604.2 1.7 subtract_bitcast_fusion
  605.9 0.8 copy.12
  607.7 1.1 fusion.32
  609.2 5.0 while.21
  613.4 0.7 fusion.63
  614.2 0.8 collective-permute-start.1
  615.0 5.0 while.20
  620.0 4.5 convolution_convert_fusion.2
  624.5 141.9 %reduce-scatter.2.cloned.1.call-done = bf16[32,3072]{1,0:T(8,128)(2,1)} async-done(((bf16[1024,3072]{1,0:T(8,128)(2,1)}), bf16[32,3072]{1,0:T(8,128)(2,1)}) %reduce-scatter.2.cloned.1.call-update) | async-done | bytes 196624 | tf_op jit(solution)/shard_map/reduce_scatter | solution.py:110
  766.4 1.7 fusion.33
  (54 shorter events, 13.0 us)
Async XLA Ops:
  6.5 613.4 %copy-start = (bf16[1,2,128,3072]{3,2,1,0:T(8,128)(2,1)S(1)}, bf16[1,2,128,3072]{3,2,1,0:T(8,128)(2,1)}, u32[]{:S(2)}) copy-start(bf16[1,2,128,3072]{3,2,1,0:T(8,128)(2,1)} %param.17) | copy-start | bytes 4718596
  14.2 577.6 %all-to-all-start = ((bf16[32,32,3072]{2,1,0:T(8,128)(2,1)}), bf16[32,32,3072]{2,1,0:T(8,128)(2,1)}, u32[]{:S(2)}, u32[]{:S(2)}) async-start(bf16[32,32,3072]{2,1,0:T(8,128)(2,1)} %tile.2), calls=%async_computation | async-start | bytes 12582912 | tf_op jit(solution)/shard_map/all_to_all | solution.py:15
  46.9 719.5 %reduce-scatter.2.cloned.1.call-start = ((), (), s32[]{:S(2)}) async-start(), calls=%async_computation.2 | async-start | bytes 6488064 | tf_op jit(solution)/shard_map/reduce_scatter | solution.py:110
  51.0 4.7 copy-start.3
  51.0 4.7 copy-start.4
  51.0 5.4 copy-start.5
  598.3 1.4 copy-start.2
  607.1 1.8 collective-permute-start
  614.2 5.8 collective-permute-start.1
  624.4 142.0 %copy-start.1 = (bf16[1,32,3072]{2,1,0:T(8,128)(2,1)S(1)}, bf16[1,32,3072]{2,1,0:T(8,128)(2,1)}, u32[]{:S(2)}) copy-start(bf16[1,32,3072]{2,1,0:T(8,128)(2,1)} %param.11) | copy-start | bytes 589828
Sparse Core Ops, SparseCore 0:
  624.6 141.7 reduce-scatter.1
